TPU v7x, 32 devices: a whole 2x2x4 slice. The times are simulated.
32 devices in a mesh: row: 2 (over x), col: 4 (over y, core), layer: 4 (over z).
Axes of the slice: x: 2, y: 2, z: 4, core: 2. Of those that a mesh axis runs over, the one named last changes fastest.
Arguments:
- object_field: float32 [2, 512, 1024], P(None, 'row', 'col'), may hold values from -6 to 6
- probe_modes: float32 [2, 4, 256, 256], replicated, may hold values from -6 to 6
- amplitudes: float32 [32, 256, 256], P(('row', 'col', 'layer')), may hold values from 0 to 4
- offsets: int32 [32, 2], P(('row', 'col', 'layer')), may hold values from 0 to 768, as said below
Outputs:
- new_object: float32 [2, 512, 1024], P(None, 'row', 'col')
Inputs may be any that keep to these rules, and one draw needn't show every extreme that they name: `offsets`: every patch lies inside the 512 x 1024 object. A position held by the device at tile (r, c) has its corner inside that tile: rows r * 256 to (r + 1) * 256 - 1 and columns c * 256 to (c + 1) * 256 - 1. On a device whose tile row is not the last, its first position's patch reaches into the next tile row.
All inputs are finite; a program needn't handle non-finite values.
Results may differ from a plain program's by a relative error of at most 0.0001.
Values sent between devices are 32-bit elements; how exact they have to be, the bound alone decides.
A program may use at most 64 MiB of HBM per device.

v0:
```python
import functools

import jax
import jax.numpy as jnp
import numpy as np
from jax import lax
from jax.experimental import pallas as pl
from jax.experimental.pallas import tpu as pltpu
from jax.sharding import PartitionSpec as P

SOFTEN = 0.05
DAMPING = 0.5
AXES = ("row", "col", "layer")
PIECES = 4


def place():
    return tuple(lax.axis_index(a) for a in AXES)


def send(src, dst, send_sem, recv_sem, device):
    return pltpu.make_async_remote_copy(
        src_ref=src,
        dst_ref=dst,
        send_sem=send_sem,
        recv_sem=recv_sem,
        device_id=device,
        device_id_type=pl.DeviceIdType.MESH,
    )


def greet(rows, cols, layers):
    r, c, l = place()
    barrier = pltpu.get_barrier_semaphore()

    def tell(device):
        pl.semaphore_signal(
            barrier, inc=1, device_id=device, device_id_type=pl.DeviceIdType.MESH
        )

    near = (
        (c > 0, (r, c - 1, l)),
        (c < cols - 1, (r, c + 1, l)),
        (r > 0, (r - 1, c, l)),
        (r < rows - 1, (r + 1, c, l)),
    )
    for there, device in near:
        pl.when(there)(functools.partial(tell, device))
    for d in range(1, layers):
        tell((r, c, lax.rem(l + d, layers)))
    count = layers - 1
    for there, _ in near:
        count += there.astype(jnp.int32)
    pl.semaphore_wait(barrier, count)


def halo_kernel(
    sizes, corner, obj, off, merged, offs, right, below, diag,
    s_right, r_right, s_below, r_below, s_diag, r_diag, s_off, r_off, s_pass, r_pass,
):
    rows, cols, layers = sizes
    side = obj.shape[1]
    step = side // PIECES
    r, c, l = place()
    has_right, has_left = c < cols - 1, c > 0
    has_below, has_above = r < rows - 1, r > 0
    greet(rows, cols, layers)

    def piece(ref, k):
        return ref.at[:, pl.ds(k * step, step), :]

    to_left = send(obj, right, s_right, r_right, (r, c - 1, l))
    pl.when(has_left)(to_left.start)
    ups = [
        send(piece(obj, k), piece(below, k), s_below.at[k], r_below.at[k], (r - 1, c, l))
        for k in range(PIECES)
    ]
    for up in ups:
        pl.when(has_above)(up.start)
    mine = offs.at[0, pl.ds(l, 1)]
    peers = [
        send(off, mine, s_off.at[d], r_off.at[d], (r, c, lax.rem(l + d, layers)))
        for d in range(1, layers)
    ]
    for peer in peers:
        peer.start()
    offs[0, pl.ds(l, 1)] = off[...]
    for peer in peers:
        peer.wait()
    across = send(offs.at[0], offs.at[1], s_pass.at[0], r_pass.at[0], (r, c + 1, l))
    pl.when(has_right)(across.start)

    diags = [
        send(piece(below, k), piece(diag, k), s_diag.at[k], r_diag.at[k], (r, c - 1, l))
        for k in range(PIECES)
    ]

    def forward(k):
        @pl.when(has_below)
        def _():
            ups[k].wait_recv()
            pl.when(has_left)(diags[k].start)

    forward(0)
    down0 = send(offs.at[0], offs.at[2], s_pass.at[1], r_pass.at[1], (r + 1, c, l))
    down1 = send(offs.at[1], offs.at[3], s_pass.at[2], r_pass.at[2], (r + 1, c, l))
    pl.when(has_left)(across.wait_recv)

    @pl.when(has_below)
    def _():
        down0.start()
        pl.when(has_left)(down1.start)

    for k in range(1, PIECES):
        forward(k)

    base_row, base_col = corner[0, 0] - r * side, corner[0, 1] - c * side
    pl.when(has_right)(to_left.wait_recv)
    lane = lax.broadcasted_iota(jnp.int32, (step, side), 1)
    line = lax.broadcasted_iota(jnp.int32, (step, side), 0)
    for k in range(PIECES):
        part = pl.ds(k * step, step)
        for h in range(2):
            merged[h, part, :] = obj[h, part, :]

        @pl.when(has_right)
        def _():
            for h in range(2):
                merged[h, part, :] = jnp.where(
                    lane < base_col, right[h, part, :], merged[h, part, :]
                )

        @pl.when(has_below)
        def _():
            for h in range(2):
                merged[h, part, :] = jnp.where(
                    (line + k * step < base_row) & (lane >= base_col),
                    below[h, part, :],
                    merged[h, part, :],
                )

        @pl.when(has_below & has_right)
        def _():
            diags[k].wait_recv()
            for h in range(2):
                merged[h, part, :] = jnp.where(
                    (line + k * step < base_row) & (lane < base_col),
                    diag[h, part, :],
                    merged[h, part, :],
                )

    @pl.when(jnp.logical_not(has_left))
    def _():
        offs[1] = jnp.zeros(offs.shape[1:], jnp.int32)

    @pl.when(jnp.logical_not(has_above))
    def _():
        offs[2] = jnp.zeros(offs.shape[1:], jnp.int32)

    @pl.when(jnp.logical_not(has_above & has_left))
    def _():
        offs[3] = jnp.zeros(offs.shape[1:], jnp.int32)

    pl.when(has_left)(to_left.wait_send)
    pl.when(has_right)(across.wait_send)

    @pl.when(has_above)
    def _():
        for up in ups:
            up.wait_send()
        down0.wait_recv()
        pl.when(has_left)(down1.wait_recv)

    @pl.when(has_below)
    def _():
        down0.wait_send()

        @pl.when(has_left)
        def _():
            down1.wait_send()
            for copy in diags:
                copy.wait_send()


def split(x):
    high = x.astype(jnp.bfloat16)
    return high, (x - high.astype(jnp.float32)).astype(jnp.bfloat16)


def prod(left, right):
    def one(a, b):
        return jnp.dot(a, b, preferred_element_type=jnp.float32)

    return one(left[0], right[0]) + (one(left[0], right[1]) + one(left[1], right[0]))


def wave_kernel(
    sizes, corner, offs, merged, probe, amp, fwd_high, fwd_low, inv_high, inv_low,
    terms, weight, rolled, far, ratio, power, twice,
):
    layers = sizes[2]
    share = merged.shape[1] // layers
    side = merged.shape[1]
    modes = probe.shape[1]
    r, c, l = place()
    has_left, has_above = c > 0, r > 0
    down, over = corner[0, 0] - r * side, corner[0, 1] - c * side
    fwd = (fwd_high, fwd_low)
    inv = (inv_high, inv_low)

    def last(x, table):
        return prod(split(x), (table[0][...], table[1][...]))

    def first(table, x):
        a = (table[0][:, :side], table[1][:, :side])
        b = (table[0][:, side:], table[1][:, side:])
        return prod(a, split(x[:, :side])) + prod(b, split(x[:, side:]))

    ratio[...] = jnp.zeros_like(ratio)
    power[...] = jnp.zeros_like(power)

    def forward(m, carry):
        plain = probe[0, m], probe[1, m]
        power[...] += plain[0] * plain[0] + plain[1] * plain[1]
        real, imag = (pltpu.roll(pltpu.roll(x, down, 0), over, 1) for x in plain)
        rolled[0, m] = real
        rolled[1, m] = imag
        exit_wave = jnp.concatenate(
            [real * merged[0] - imag * merged[1], real * merged[1] + imag * merged[0]], axis=1
        )
        spread = first(inv, last(exit_wave, fwd))
        far[m] = spread
        ratio[...] += spread[:side] * spread[:side] + spread[side:] * spread[side:]
        return carry

    lax.fori_loop(0, modes, forward, 0)
    ratio[...] = amp[0] / (jnp.sqrt(ratio[...]) + SOFTEN)
    terms[...] = jnp.zeros_like(terms)

    def backward(m, carry):
        scale = ratio[...]
        fixed = jnp.concatenate([far[m, :side] * scale, far[m, side:] * scale], axis=1)
        back = first(fwd, fixed)
        back = last(jnp.concatenate([back[:side], back[side:]], axis=1), inv)
        new_real, new_imag = back[:, :side], back[:, side:]
        real, imag = rolled[0, m], rolled[1, m]
        terms[0] += real * new_real + imag * new_imag
        terms[1] += real * new_imag - imag * new_real
        return carry

    lax.fori_loop(0, modes, backward, 0)

    twice[:side, :] = power[...]
    twice[side : 2 * side, :] = power[...]
    twice[2 * side :, :] = jnp.zeros((8, side), jnp.float32)
    lane = lax.broadcasted_iota(jnp.int32, (share, side), 1)
    at = lax.broadcasted_iota(jnp.int32, (share, side), 0) + l * share
    total = jnp.zeros((share, side), jnp.float32)
    there = (None, has_left, has_above, has_left & has_above)
    for group in range(4):
        for layer in range(layers):
            a, b = corner_of(offs, group, layer, side)
            a = jnp.clip(a, 0, side)
            b = jnp.clip(b, 0, side)
            start = side + l * share - a
            extra = lax.rem(start, 8)
            window = twice[pl.ds(pl.multiple_of(start - extra, 8), share + 8), :]
            window = pltpu.roll(window, lax.rem(share + 8 - extra, share + 8), 0)[:share]
            window = pltpu.roll(window, lax.rem(b, side), 1)
            keep = (at < a) if group >= 2 else (at >= a)
            keep &= (lane < b) if group % 2 else (lane >= b)
            if there[group] is not None:
                keep &= there[group]
            total += jnp.where(keep, window, 0.0)
    weight[...] = total + DAMPING


def corner_of(offs, group, layer, side):
    r, c, _ = place()
    tile_row = r - (1 if group >= 2 else 0)
    tile_col = c - (group % 2)
    return offs[group, layer, 0] - tile_row * side, offs[group, layer, 1] - tile_col * side


def sum_kernel(
    sizes, offs, terms, weight, obj, out,
    left, own, lower, upper, shares, s_left, r_left, s_down, r_down, s_rs, r_rs, s_ag, r_ag,
):
    rows, cols, layers = sizes
    side = obj.shape[1]
    step = side // PIECES
    share = side // layers
    r, c, l = place()
    has_right, has_left = c < cols - 1, c > 0
    has_below, has_above = r < rows - 1, r > 0
    greet(rows, cols, layers)

    def piece(ref, k):
        return ref.at[:, pl.ds(k * step, step), :]

    rights = [
        send(piece(terms, k), piece(left, k), s_left.at[k], r_left.at[k], (r, c + 1, l))
        for k in range(PIECES)
    ]
    for copy in rights:
        pl.when(has_right)(copy.start)
    downs = [
        send(piece(lower, k), piece(upper, k), s_down.at[k], r_down.at[k], (r + 1, c, l))
        for k in range(PIECES)
    ]
    spreads = []
    for d in range(1, layers):
        peer = lax.rem(l + d, layers)
        spreads.append(
            (
                peer,
                send(
                    own.at[:, pl.ds(peer * share, share), :],
                    shares.at[d],
                    s_rs.at[d],
                    r_rs.at[d],
                    (r, c, peer),
                ),
            )
        )

    lane = lax.broadcasted_iota(jnp.int32, (step, side), 1)
    line = lax.broadcasted_iota(jnp.int32, (step, side), 0)
    down, over = corner_of(offs, 0, l, side)
    left_down, left_over = corner_of(offs, 1, l, side)
    for k in range(PIECES):
        part = pl.ds(k * step, step)
        at = line + k * step
        for h in range(2):
            mine = jnp.where(lane >= over, terms[h, part, :], 0.0)
            own[h, part, :] = jnp.where(at >= down, mine, 0.0)
            lower[h, part, :] = jnp.where(at < down, mine, 0.0)

        @pl.when(has_left)
        def _():
            rights[k].wait_recv()
            for h in range(2):
                other = jnp.where(lane < left_over, left[h, part, :], 0.0)
                own[h, part, :] += jnp.where(at >= left_down, other, 0.0)
                lower[h, part, :] += jnp.where(at < left_down, other, 0.0)

        pl.when(has_below)(downs[k].start)

        @pl.when(jnp.logical_not(has_above))
        def _():
            for peer, copy in spreads:
                pl.when(peer * share // step == k)(copy.start)

    @pl.when(has_above)
    def _():
        for k in range(PIECES):
            part = pl.ds(k * step, step)
            downs[k].wait_recv()
            for h in range(2):
                own[h, part, :] += upper[h, part, :]
            for peer, copy in spreads:
                pl.when(peer * share // step == k)(copy.start)

    strip = pl.ds(pl.multiple_of(l * share, share), share)
    for _, copy in spreads:
        copy.wait_recv()
    for h in range(2):
        number = own[h, strip, :] + DAMPING * obj[h, strip, :]
        for d in range(1, layers):
            number += shares[d, h]
        out[h, strip, :] = number / weight[...]
    gathers = [
        send(
            out.at[:, strip, :],
            out.at[:, strip, :],
            s_ag.at[d],
            r_ag.at[d],
            (r, c, lax.rem(l + d, layers)),
        )
        for d in range(1, layers)
    ]
    for copy in gathers:
        copy.start()
    for copy in gathers:
        copy.wait()
    for _, copy in spreads:
        copy.wait_send()

    @pl.when(has_right)
    def _():
        for copy in rights:
            copy.wait_send()

    @pl.when(has_below)
    def _():
        for copy in downs:
            copy.wait_send()


def tables(side):
    steps = np.arange(side)
    angle = (steps[:, None] * steps[None, :] % side) * (2.0 * np.pi / side)
    real, imag = np.cos(angle) / np.sqrt(side), -np.sin(angle) / np.sqrt(side)
    both = np.block([[real, imag], [-imag, real]])

    def halves(x):
        x = x.astype(np.float32)
        high = x.astype(jnp.bfloat16)
        return high, (x - high.astype(np.float32)).astype(jnp.bfloat16)

    return halves(both) + halves(both.T)


def body(sizes, object_field, probe_modes, amplitudes, offsets):
    rows, cols, layers = sizes
    side = object_field.shape[1]
    assert object_field.shape[2] == side and probe_modes.shape[2] == side
    assert offsets.shape[0] == 1 and side % (8 * layers) == 0
    modes = probe_modes.shape[1]
    vmem = pl.BlockSpec(memory_space=pltpu.VMEM)
    smem = pl.BlockSpec(memory_space=pltpu.SMEM)
    pair = (2, side, side)
    f32 = jnp.float32
    dma = pltpu.SemaphoreType.DMA
    off = jnp.pad(offsets.reshape(1, 1, 2), ((0, 0), (0, 0), (0, 126)))
    off = jnp.broadcast_to(off, (1, 8, 128))
    merged, offs = pl.pallas_call(
        functools.partial(halo_kernel, sizes),
        out_shape=(
            jax.ShapeDtypeStruct(pair, f32),
            jax.ShapeDtypeStruct((4, layers, 8, 128), jnp.int32),
        ),
        in_specs=[smem, vmem, vmem],
        out_specs=(vmem, vmem),
        scratch_shapes=[pltpu.VMEM(pair, f32)] * 3
        + [dma(()), dma(())]
        + [dma((PIECES,))] * 4
        + [dma((layers,))] * 2
        + [dma((3,))] * 2,
        compiler_params=pltpu.CompilerParams(collective_id=0, has_side_effects=True),
        name="halo",
    )(offsets, object_field, off)
    corners = offs[:, :, 0, :2]
    terms, weight = pl.pallas_call(
        functools.partial(wave_kernel, sizes),
        out_shape=(
            jax.ShapeDtypeStruct(pair, f32),
            jax.ShapeDtypeStruct((side // layers, side), f32),
        ),
        in_specs=[smem, smem] + [vmem] * 7,
        out_specs=(vmem, vmem),
        scratch_shapes=[
            pltpu.VMEM((2, modes, side, side), f32),
            pltpu.VMEM((modes, 2 * side, side), f32),
            pltpu.VMEM((side, side), f32),
            pltpu.VMEM((side, side), f32),
            pltpu.VMEM((2 * side + 8, side), f32),
        ],
        name="wave",
    )(offsets, corners, merged, probe_modes, amplitudes, *(jnp.asarray(t) for t in tables(side)))
    return pl.pallas_call(
        functools.partial(sum_kernel, sizes),
        out_shape=jax.ShapeDtypeStruct(pair, f32),
        in_specs=[smem] + [vmem] * 3,
        out_specs=vmem,
        scratch_shapes=[pltpu.VMEM(pair, f32)] * 4
        + [pltpu.VMEM((layers, 2, side // layers, side), f32)]
        + [dma((PIECES,))] * 4
        + [dma((layers,))] * 4,
        compiler_params=pltpu.CompilerParams(collective_id=1, has_side_effects=True),
        name="sums",
    )(corners, terms, weight, object_field)


def solution(mesh):
    sizes = tuple(mesh.shape[a] for a in AXES)
    placed = (
        P(None, "row", "col"),
        P(),
        P(("row", "col", "layer"), None, None),
        P(("row", "col", "layer"), None),
    )
    return jax.shard_map(
        functools.partial(body, sizes),
        mesh=mesh,
        in_specs=placed,
        out_specs=P(None, "row", "col"),
        check_vma=False,
    )
```

profile of v0, /device:TPU:19, one launch (start us, length us, event | category | flops | bytes accessed | tf_op | source)
XLA Modules:
  0.0 85.2 jit_solution(1822083588196490306)
XLA Ops:
  0.0 0.7 pad_bitcast_fusion
  0.7 0.6 broadcast_in_dim.8.off
  1.3 15.0 %halo.1 = (f32[2,256,256]{2,1,0:T(8,128)}, s32[4,4,8,128]{3,2,1,0:T(8,128)}) custom-call(s32[1,2]{1,0:T(1,128)} %corner.3, f32[2,256,256]{2,1,0:T(8,128)} %obj.3, s32[1,8,128]{2,1,0:T(8,128)} %broadcast_in_dim.8.off), custom_call_target="tpu_custom_call" | custom-call | tf_op jit(solution)/shard_map/halo/pallas_call | solution.py:427
  16.3 1.4 %slice.3 = s32[4,4,1,2]{3,2,1,0:T(1,128)} slice(s32[4,4,8,128]{3,2,1,0:T(8,128)} %get-tuple-element.9), slice={[0:4], [0:4], [0:1], [0:2]} | slice | bytes 256 | tf_op jit(solution)/shard_map/slice | solution.py:443
  17.7 16.5 %wave.1 = (f32[2,256,256]{2,1,0:T(8,128)}, f32[64,256]{1,0:T(8,128)}) custom-call(s32[1,2]{1,0:T(1,128)} %corner.3, s32[4,4,2]{2,1,0:T(4,128)} %bitcast.4, f32[2,256,256]{2,1,0:T(8,128)} %get-tuple-element.10.merged, f32[2,4,256,256]{3,2,1,0:T(8,128)} %probe.1, f32[1,256,256]{2,1,0:T(8,128)} %amp.1, bf16[512,512]{1,0:T(8,128)(2,1)} %constant.10.clone.fwd_high, ...), custom_call_target="tpu_custom_call" | custom-call | tf_op jit(solution)/shard_map/wave/pallas_call | solution.py:444
  34.2 49.1 %sums.1 = f32[2,256,256]{2,1,0:T(8,128)} custom-call(s32[4,4,2]{2,1,0:T(4,128)} %bitcast.5, f32[2,256,256]{2,1,0:T(8,128)} %get-tuple-element.11.terms, f32[64,256]{1,0:T(8,128)} %get-tuple-element.12.weight, f32[2,256,256]{2,1,0:T(8,128)} %obj.3), custom_call_target="tpu_custom_call" | custom-call | tf_op jit(solution)/shard_map/sums/pallas_call | solution.py:461
  83.3 1.9 %copy.14 = f32[2,256,256]{2,1,0:T(8,128)} copy(f32[2,256,256]{2,1,0:T(8,128)} %sums.1) | data formatting | bytes 1048576
where the time goes:
time: 85.5 us; the launch traced here: 85.2 us
  Pallas kernels  80.6 us (94%)
  local copies, waits for them, and re-layouts  4.56 us (5%)
    pallas_call x1, Pallas kernels, body(): pl.pallas_call(functools.partial(sum_kernel, sizes), out_shape=jax.ShapeD...  49.1 us
    pallas_call x1, Pallas kernels, body(): pl.pallas_call(functools.partial(wave_kernel, sizes), out_shape=(jax.Shap...  16.5 us
    pallas_call x1, Pallas kernels, body(): pl.pallas_call(functools.partial(halo_kernel, sizes), out_shape=(jax.Shap...  15 us
    unnamed x1, local copies, waits for them, and re-layouts  1.87 us

commit v1 on v0

--- a/solution.py
+++ b/solution.py
@@ -55,7 +55,7 @@
 
 
 def halo_kernel(
-    sizes, corner, obj, off, merged, offs, right, below, diag,
+    sizes, corner, obj, merged, offs, right, below, diag,
     s_right, r_right, s_below, r_below, s_diag, r_diag, s_off, r_off, s_pass, r_pass,
 ):
     rows, cols, layers = sizes
@@ -64,6 +64,8 @@
     r, c, l = place()
     has_right, has_left = c < cols - 1, c > 0
     has_below, has_above = r < rows - 1, r > 0
+    at = lax.broadcasted_iota(jnp.int32, (1, 1, 128), 2)
+    offs[0, pl.ds(l, 1)] = jnp.where(at == 0, corner[0, 0], corner[0, 1])
     greet(rows, cols, layers)
 
     def piece(ref, k):
@@ -79,12 +81,11 @@
         pl.when(has_above)(up.start)
     mine = offs.at[0, pl.ds(l, 1)]
     peers = [
-        send(off, mine, s_off.at[d], r_off.at[d], (r, c, lax.rem(l + d, layers)))
+        send(mine, mine, s_off.at[d], r_off.at[d], (r, c, lax.rem(l + d, layers)))
         for d in range(1, layers)
     ]
     for peer in peers:
         peer.start()
-    offs[0, pl.ds(l, 1)] = off[...]
     for peer in peers:
         peer.wait()
     across = send(offs.at[0], offs.at[1], s_pass.at[0], r_pass.at[0], (r, c + 1, l))
@@ -279,7 +280,7 @@
     r, c, _ = place()
     tile_row = r - (1 if group >= 2 else 0)
     tile_col = c - (group % 2)
-    return offs[group, layer, 0] - tile_row * side, offs[group, layer, 1] - tile_col * side
+    return offs[group, layer, 0, 0] - tile_row * side, offs[group, layer, 0, 1] - tile_col * side
 
 
 def sum_kernel(
@@ -287,104 +288,113 @@
     left, own, lower, upper, shares, s_left, r_left, s_down, r_down, s_rs, r_rs, s_ag, r_ag,
 ):
     rows, cols, layers = sizes
-    side = obj.shape[1]
-    step = side // PIECES
-    share = side // layers
+    share, side = obj.shape[2], obj.shape[3]
+    count = s_left.shape[0]
+    step = share // count
     r, c, l = place()
     has_right, has_left = c < cols - 1, c > 0
     has_below, has_above = r < rows - 1, r > 0
+    parts = [pl.ds(k * step, step) for k in range(count)]
     greet(rows, cols, layers)
 
-    def piece(ref, k):
-        return ref.at[:, pl.ds(k * step, step), :]
-
-    rights = [
-        send(piece(terms, k), piece(left, k), s_left.at[k], r_left.at[k], (r, c + 1, l))
-        for k in range(PIECES)
-    ]
+    rights, downs, spreads, gathers = [], [], [], []
+    for k, part in enumerate(parts):
+        rights.append(
+            send(
+                terms.at[:, :, part], left.at[:, :, part], s_left.at[k], r_left.at[k], (r, c + 1, l)
+            )
+        )
+        downs.append(
+            send(
+                lower.at[:, :, part], upper.at[:, :, part], s_down.at[k], r_down.at[k], (r + 1, c, l)
+            )
+        )
+        peers = [(d, lax.rem(l + d, layers)) for d in range(1, layers)]
+        spreads.append(
+            [
+                send(
+                    own.at[:, peer, part], shares.at[d, :, part],
+                    s_rs.at[k, d], r_rs.at[k, d], (r, c, peer),
+                )
+                for d, peer in peers
+            ]
+        )
+        gathers.append(
+            [
+                send(
+                    out.at[:, l, part], out.at[:, l, part],
+                    s_ag.at[k, d], r_ag.at[k, d], (r, c, peer),
+                )
+                for d, peer in peers
+            ]
+        )
     for copy in rights:
         pl.when(has_right)(copy.start)
-    downs = [
-        send(piece(lower, k), piece(upper, k), s_down.at[k], r_down.at[k], (r + 1, c, l))
-        for k in range(PIECES)
-    ]
-    spreads = []
-    for d in range(1, layers):
-        peer = lax.rem(l + d, layers)
-        spreads.append(
-            (
-                peer,
-                send(
-                    own.at[:, pl.ds(peer * share, share), :],
-                    shares.at[d],
-                    s_rs.at[d],
-                    r_rs.at[d],
-                    (r, c, peer),
-                ),
-            )
-        )
-
-    lane = lax.broadcasted_iota(jnp.int32, (step, side), 1)
-    line = lax.broadcasted_iota(jnp.int32, (step, side), 0)
+
+    shape = (layers, step, side)
+    lane = lax.broadcasted_iota(jnp.int32, shape, 2)
+    line = lax.broadcasted_iota(jnp.int32, shape, 0) * share
+    line += lax.broadcasted_iota(jnp.int32, shape, 1)
     down, over = corner_of(offs, 0, l, side)
     left_down, left_over = corner_of(offs, 1, l, side)
-    for k in range(PIECES):
-        part = pl.ds(k * step, step)
+
+    def finish(k):
+        part = parts[k]
+        for copy in spreads[k]:
+            copy.wait_recv()
+        for h in range(2):
+            number = own[h, l, part, :] + DAMPING * obj[h, l, part, :]
+            for d in range(1, layers):
+                number += shares[d, h, part, :]
+            out[h, l, part, :] = number / weight[part, :]
+        for copy in gathers[k]:
+            copy.start()
+
+    for k, part in enumerate(parts):
         at = line + k * step
         for h in range(2):
-            mine = jnp.where(lane >= over, terms[h, part, :], 0.0)
-            own[h, part, :] = jnp.where(at >= down, mine, 0.0)
-            lower[h, part, :] = jnp.where(at < down, mine, 0.0)
+            mine = jnp.where(lane >= over, terms[h, :, part, :], 0.0)
+            own[h, :, part, :] = jnp.where(at >= down, mine, 0.0)
+            lower[h, :, part, :] = jnp.where(at < down, mine, 0.0)
 
         @pl.when(has_left)
         def _():
             rights[k].wait_recv()
             for h in range(2):
-                other = jnp.where(lane < left_over, left[h, part, :], 0.0)
-                own[h, part, :] += jnp.where(at >= left_down, other, 0.0)
-                lower[h, part, :] += jnp.where(at < left_down, other, 0.0)
+                other = jnp.where(lane < left_over, left[h, :, part, :], 0.0)
+                own[h, :, part, :] += jnp.where(at >= left_down, other, 0.0)
+                lower[h, :, part, :] += jnp.where(at < left_down, other, 0.0)
 
         pl.when(has_below)(downs[k].start)
 
         @pl.when(jnp.logical_not(has_above))
         def _():
-            for peer, copy in spreads:
-                pl.when(peer * share // step == k)(copy.start)
+            for copy in spreads[k]:
+                copy.start()
 
     @pl.when(has_above)
     def _():
-        for k in range(PIECES):
-            part = pl.ds(k * step, step)
+        for k, part in enumerate(parts):
             downs[k].wait_recv()
             for h in range(2):
-                own[h, part, :] += upper[h, part, :]
-            for peer, copy in spreads:
-                pl.when(peer * share // step == k)(copy.start)
-
-    strip = pl.ds(pl.multiple_of(l * share, share), share)
-    for _, copy in spreads:
-        copy.wait_recv()
-    for h in range(2):
-        number = own[h, strip, :] + DAMPING * obj[h, strip, :]
-        for d in range(1, layers):
-            number += shares[d, h]
-        out[h, strip, :] = number / weight[...]
-    gathers = [
-        send(
-            out.at[:, strip, :],
-            out.at[:, strip, :],
-            s_ag.at[d],
-            r_ag.at[d],
-            (r, c, lax.rem(l + d, layers)),
-        )
-        for d in range(1, layers)
-    ]
-    for copy in gathers:
-        copy.start()
-    for copy in gathers:
-        copy.wait()
-    for _, copy in spreads:
-        copy.wait_send()
+                own[h, :, part, :] += upper[h, :, part, :]
+            for copy in spreads[k]:
+                copy.start()
+            if k >= 2:
+                finish(k - 2)
+        for k in range(max(count - 2, 0), count):
+            finish(k)
+
+    @pl.when(jnp.logical_not(has_above))
+    def _():
+        for k in range(count):
+            finish(k)
+
+    for k in range(count):
+        for copy in gathers[k]:
+            copy.wait()
+        for copy in spreads[k]:
+            copy.wait_send()
 
     @pl.when(has_right)
     def _():
@@ -422,15 +432,13 @@
     pair = (2, side, side)
     f32 = jnp.float32
     dma = pltpu.SemaphoreType.DMA
-    off = jnp.pad(offsets.reshape(1, 1, 2), ((0, 0), (0, 0), (0, 126)))
-    off = jnp.broadcast_to(off, (1, 8, 128))
     merged, offs = pl.pallas_call(
         functools.partial(halo_kernel, sizes),
         out_shape=(
             jax.ShapeDtypeStruct(pair, f32),
-            jax.ShapeDtypeStruct((4, layers, 8, 128), jnp.int32),
+            jax.ShapeDtypeStruct((4, layers, 1, 128), jnp.int32),
         ),
-        in_specs=[smem, vmem, vmem],
+        in_specs=[smem, vmem],
         out_specs=(vmem, vmem),
         scratch_shapes=[pltpu.VMEM(pair, f32)] * 3
         + [dma(()), dma(())]
@@ -439,8 +447,7 @@
         + [dma((3,))] * 2,
         compiler_params=pltpu.CompilerParams(collective_id=0, has_side_effects=True),
         name="halo",
-    )(offsets, object_field, off)
-    corners = offs[:, :, 0, :2]
+    )(offsets, object_field)
     terms, weight = pl.pallas_call(
         functools.partial(wave_kernel, sizes),
         out_shape=(
@@ -457,19 +464,23 @@
             pltpu.VMEM((2 * side + 8, side), f32),
         ],
         name="wave",
-    )(offsets, corners, merged, probe_modes, amplitudes, *(jnp.asarray(t) for t in tables(side)))
-    return pl.pallas_call(
+    )(offsets, offs, merged, probe_modes, amplitudes, *(jnp.asarray(t) for t in tables(side)))
+    share = side // layers
+    count = min(PIECES, share // 8)
+    cut = (2, layers, share, side)
+    new_object = pl.pallas_call(
         functools.partial(sum_kernel, sizes),
-        out_shape=jax.ShapeDtypeStruct(pair, f32),
+        out_shape=jax.ShapeDtypeStruct(cut, f32),
         in_specs=[smem] + [vmem] * 3,
         out_specs=vmem,
-        scratch_shapes=[pltpu.VMEM(pair, f32)] * 4
-        + [pltpu.VMEM((layers, 2, side // layers, side), f32)]
-        + [dma((PIECES,))] * 4
-        + [dma((layers,))] * 4,
+        scratch_shapes=[pltpu.VMEM(cut, f32)] * 4
+        + [pltpu.VMEM((layers, 2, share, side), f32)]
+        + [dma((count,))] * 4
+        + [dma((count, layers))] * 4,
         compiler_params=pltpu.CompilerParams(collective_id=1, has_side_effects=True),
         name="sums",
-    )(corners, terms, weight, object_field)
+    )(offs, terms.reshape(cut), weight, object_field.reshape(cut))
+    return new_object.reshape(pair)
 
 
 def solution(mesh):

time: 85.5 us -> 75.4 us (0.88)
  the two profiles are of different devices: /device:TPU:19 before, /device:TPU:6 now
where the time goes in v1:
time: 75.4 us; the launch traced here: 75.2 us
  Pallas kernels  73.3 us (97%)
  local copies, waits for them, and re-layouts  1.87 us (2%)
    pallas_call x1, Pallas kernels, body(): pl.pallas_call(functools.partial(sum_kernel, sizes), out_shape=jax.ShapeD...  39.8 us
    pallas_call x1, Pallas kernels, body(): pl.pallas_call(functools.partial(halo_kernel, sizes), out_shape=(jax.Shap...  17 us
    pallas_call x1, Pallas kernels, body(): pl.pallas_call(functools.partial(wave_kernel, sizes), out_shape=(jax.Shap...  16.5 us
    unnamed x1, local copies, waits for them, and re-layouts  1.87 us

profile of v1, /device:TPU:6, one launch (start us, length us, event | category | flops | bytes accessed | tf_op | source)
XLA Modules:
  0.0 75.2 jit_solution(16182423039809021232)
XLA Ops:
  0.0 17.0 %halo.1 = (f32[2,256,256]{2,1,0:T(8,128)}, s32[4,4,1,128]{3,2,1,0:T(1,128)}) custom-call(s32[1,2]{1,0:T(1,128)} %corner.3, f32[2,256,256]{2,1,0:T(8,128)} %obj.1), custom_call_target="tpu_custom_call" | custom-call | tf_op jit(solution)/shard_map/halo/pallas_call | solution.py:435
  17.0 16.5 %wave.1 = (f32[2,256,256]{2,1,0:T(8,128)}, f32[64,256]{1,0:T(8,128)}) custom-call(s32[1,2]{1,0:T(1,128)} %corner.3, s32[4,4,1,128]{3,2,1,0:T(1,128)} %get-tuple-element.9.offs, f32[2,256,256]{2,1,0:T(8,128)} %get-tuple-element.10.merged, f32[2,4,256,256]{3,2,1,0:T(8,128)} %probe.1, f32[1,256,256]{2,1,0:T(8,128)} %amp.1, ...), custom_call_target="tpu_custom_call" | custom-call | tf_op jit(solution)/shard_map/wave/pallas_call | solution.py:451
  33.5 39.8 %sums.1 = f32[2,4,64,256]{3,2,1,0:T(8,128)} custom-call(s32[4,4,1,128]{3,2,1,0:T(1,128)} %get-tuple-element.9.offs, f32[2,4,64,256]{3,2,1,0:T(8,128)} %bitcast.5, f32[64,256]{1,0:T(8,128)} %get-tuple-element.12.weight, f32[2,4,64,256]{3,2,1,0:T(8,128)} %bitcast.3), custom_call_target="tpu_custom_call" | custom-call | tf_op jit(solution)/shard_map/sums/pallas_call | solution.py:471
  73.3 1.9 %copy.10 = f32[2,256,256]{2,1,0:T(8,128)} copy(f32[2,256,256]{2,1,0:T(8,128)} %bitcast.4) | data formatting | bytes 1048576

commit v2 on v1

v2 whole, which is shorter than its diff:
```python
import functools

import jax
import jax.numpy as jnp
import numpy as np
from jax import lax
from jax.experimental import pallas as pl
from jax.experimental.pallas import tpu as pltpu
from jax.sharding import PartitionSpec as P

SOFTEN = 0.05
DAMPING = 0.5
AXES = ("row", "col", "layer")
PIECES = 4
LAG = 2


def place():
    return tuple(lax.axis_index(a) for a in AXES)


def send(src, dst, send_sem, recv_sem, device):
    return pltpu.make_async_remote_copy(
        src_ref=src,
        dst_ref=dst,
        send_sem=send_sem,
        recv_sem=recv_sem,
        device_id=device,
        device_id_type=pl.DeviceIdType.MESH,
    )


def greet(rows, cols, layers):
    r, c, l = place()
    barrier = pltpu.get_barrier_semaphore()

    def tell(device):
        pl.semaphore_signal(
            barrier, inc=1, device_id=device, device_id_type=pl.DeviceIdType.MESH
        )

    near = (
        (c > 0, (r, c - 1, l)),
        (c < cols - 1, (r, c + 1, l)),
        (r > 0, (r - 1, c, l)),
        (r < rows - 1, (r + 1, c, l)),
    )
    for there, device in near:
        pl.when(there)(functools.partial(tell, device))
    for d in range(1, layers):
        tell((r, c, lax.rem(l + d, layers)))
    count = layers - 1
    for there, _ in near:
        count += there.astype(jnp.int32)
    pl.semaphore_wait(barrier, count)


def split(x):
    high = x.astype(jnp.bfloat16)
    return high, (x - high.astype(jnp.float32)).astype(jnp.bfloat16)


def prod(left, right):
    def one(a, b):
        return jnp.dot(a, b, preferred_element_type=jnp.float32)

    return one(left[0], right[0]) + (one(left[0], right[1]) + one(left[1], right[0]))


def turned(x, amount, axis):
    length = x.shape[axis]
    bit = 1
    while bit < length:
        x = jnp.where(lax.rem(lax.div(amount, bit), 2) == 1, jnp.roll(x, bit, axis), x)
        bit *= 2
    return x


def corner_of(offs, group, layer, side):
    r, c, _ = place()
    tile_row = r - (1 if group >= 2 else 0)
    tile_col = c - (group % 2)
    return offs[group, layer, 0, 0] - tile_row * side, offs[group, layer, 0, 1] - tile_col * side


def kernel(
    sizes, corner, obj, probe_hbm, amp_hbm, fwd_high_hbm, fwd_low_hbm, inv_high_hbm, inv_low_hbm,
    out,
    probe, amp, fwd_high, fwd_low, inv_high, inv_low, offs, corners,
    right, below, diag, rolled, lines, far, ratio, power, weight, rows_of,
    terms, left, own, lower, upper, shares,
    s_load, s_corner, s_off, r_off, s_pass, r_pass,
    s_right, r_right, s_below, r_below, s_diag, r_diag,
    s_left, r_left, s_down, r_down, s_rs, r_rs, s_ag, r_ag,
):
    rows, cols, layers = sizes
    share, side = obj.shape[2], obj.shape[3]
    modes = probe.shape[1]
    count = s_left.shape[0]
    step = share // count
    tall = layers * step
    r, c, l = place()
    has_right, has_left = c < cols - 1, c > 0
    has_below, has_above = r < rows - 1, r > 0
    parts = [pl.ds(k * step, step) for k in range(count)]
    down = corner[0, 0] - r * side
    over = corner[0, 1] - c * side
    loads = [
        pltpu.make_async_copy(src, dst, s_load.at[i])
        for i, (src, dst) in enumerate(
            (
                (probe_hbm, probe),
                (fwd_high_hbm, fwd_high),
                (fwd_low_hbm, fwd_low),
                (inv_high_hbm, inv_high),
                (inv_low_hbm, inv_low),
                (amp_hbm, amp),
            )
        )
    ]
    for copy in loads:
        copy.start()
    at = lax.broadcasted_iota(jnp.int32, (1, 1, 128), 2)
    offs[0, pl.ds(l, 1)] = jnp.where(at == 0, corner[0, 0], corner[0, 1])
    greet(rows, cols, layers)

    west, east = (r, c - 1, l), (r, c + 1, l)
    north, south = (r - 1, c, l), (r + 1, c, l)

    def pieces(src, dst, sems, device):
        return [
            send(src.at[:, :, part], dst.at[:, :, part], sems[0].at[k], sems[1].at[k], device)
            for k, part in enumerate(parts)
        ]

    lefts = pieces(obj, right, (s_right, r_right), west)
    ups = pieces(obj, below, (s_below, r_below), north)
    diags = pieces(below, diag, (s_diag, r_diag), west)
    for k in range(count):
        pl.when(has_left)(lefts[k].start)
        pl.when(has_above)(ups[k].start)
    mine = offs.at[0, pl.ds(l, 1)]
    around = [(d, lax.rem(l + d, layers)) for d in range(1, layers)]
    peers = [send(mine, mine, s_off.at[d], r_off.at[d], (r, c, p)) for d, p in around]
    for peer in peers:
        peer.start()
    loads[0].wait()

    def forward(k):
        @pl.when(has_below)
        def _():
            ups[k].wait_recv()
            pl.when(has_left)(diags[k].start)

    def prepare(m):
        for h in range(2):
            x = probe[h, m].reshape(side, side)
            rolled[h, m] = turned(turned(x, down, 0), over, 1).reshape(layers, share, side)

    power[...] = jnp.zeros_like(power)
    for k in range(max(modes, count)):
        if k < modes:
            prepare(k)
            real, imag = probe[0, k], probe[1, k]
            power[...] += (real * real + imag * imag).reshape(side, side)
        if k == 0:
            for peer in peers:
                peer.wait()
            across = send(offs.at[0], offs.at[1], s_pass.at[0], r_pass.at[0], east)
            pl.when(has_right)(across.start)
        if k < count:
            forward(k)

    down0 = send(offs.at[0], offs.at[2], s_pass.at[1], r_pass.at[1], south)
    down1 = send(offs.at[1], offs.at[3], s_pass.at[2], r_pass.at[2], south)
    pl.when(has_left)(across.wait_recv)

    @pl.when(has_below)
    def _():
        down0.start()
        pl.when(has_left)(down1.start)

    for copy in loads[1:]:
        copy.wait()
    fwd, inv = (fwd_high, fwd_low), (inv_high, inv_low)

    def last(x, table):
        return prod(split(x), (table[0][...], table[1][...]))

    def first(table, x):
        a = (table[0][:, :side], table[1][:, :side])
        b = (table[0][:, side:], table[1][:, side:])
        return prod(a, split(x[:, :side])) + prod(b, split(x[:, side:]))

    shape = (layers, step, side)
    lane = lax.broadcasted_iota(jnp.int32, shape, 2)
    line = lax.broadcasted_iota(jnp.int32, shape, 0) * share
    line += lax.broadcasted_iota(jnp.int32, shape, 1)

    for k, part in enumerate(parts):
        high = line + k * step < down
        for h in range(2):
            own[h, :, part, :] = obj[h, :, part, :]

        @pl.when(has_right)
        def _():
            lefts[k].wait_recv()
            for h in range(2):
                own[h, :, part, :] = jnp.where(
                    lane < over, right[h, :, part, :], own[h, :, part, :]
                )

        @pl.when(has_below)
        def _():
            for h in range(2):
                own[h, :, part, :] = jnp.where(
                    high & (lane >= over), below[h, :, part, :], own[h, :, part, :]
                )

        @pl.when(has_below & has_right)
        def _():
            diags[k].wait_recv()
            for h in range(2):
                own[h, :, part, :] = jnp.where(
                    high & (lane < over), diag[h, :, part, :], own[h, :, part, :]
                )

        patch = [own[h, :, part, :].reshape(tall, side) for h in range(2)]
        waves = []
        for m in range(modes):
            real, imag = (rolled[h, m, :, part, :].reshape(tall, side) for h in range(2))
            waves.append(
                jnp.concatenate(
                    [real * patch[0] - imag * patch[1], real * patch[1] + imag * patch[0]], axis=1
                )
            )
        half = last(jnp.concatenate(waves, axis=0), fwd)
        for m in range(modes):
            lines[m, :, part, :] = half[m * tall : (m + 1) * tall].reshape(layers, step, 2 * side)

    ratio[...] = jnp.zeros_like(ratio)

    def columns(m, carry):
        spread = first(inv, lines[m].reshape(side, 2 * side))
        far[m] = spread
        ratio[...] += spread[:side] * spread[:side] + spread[side:] * spread[side:]
        return carry

    lax.fori_loop(0, modes, columns, 0)
    ratio[...] = amp[0] / (jnp.sqrt(ratio[...]) + SOFTEN)

    def back(m, carry):
        scale = ratio[...]
        fixed = jnp.concatenate([far[m, :side] * scale, far[m, side:] * scale], axis=1)
        x = first(fwd, fixed)
        x = jnp.concatenate([x[:side], x[side:]], axis=1)
        lines[m] = x.reshape(layers, share, 2 * side)
        return carry

    lax.fori_loop(0, modes, back, 0)

    pl.when(has_above)(down0.wait_recv)
    pl.when(has_above & has_left)(down1.wait_recv)

    @pl.when(jnp.logical_not(has_left))
    def _():
        offs[1] = jnp.zeros(offs.shape[1:], jnp.int32)

    @pl.when(jnp.logical_not(has_above))
    def _():
        offs[2] = jnp.zeros(offs.shape[1:], jnp.int32)

    @pl.when(jnp.logical_not(has_above & has_left))
    def _():
        offs[3] = jnp.zeros(offs.shape[1:], jnp.int32)

    fetch = pltpu.make_async_copy(offs, corners, s_corner)
    fetch.start()
    fetch.wait()

    rights = pieces(terms, left, (s_left, r_left), east)
    downs = pieces(lower, upper, (s_down, r_down), south)
    spreads, gathers = [], []
    for k, part in enumerate(parts):
        spreads.append(
            [
                send(
                    own.at[:, p, part], shares.at[d, :, part],
                    s_rs.at[k, d], r_rs.at[k, d], (r, c, p),
                )
                for d, p in around
            ]
        )
        gathers.append(
            [
                send(
                    out.at[:, l, part], out.at[:, l, part],
                    s_ag.at[k, d], r_ag.at[k, d], (r, c, p),
                )
                for d, p in around
            ]
        )
    left_down, left_over = corner_of(corners, 1, l, side)

    def rows_back(k):
        part = parts[k]
        x = jnp.concatenate(
            [lines[m, :, part, :].reshape(tall, 2 * side) for m in range(modes)], axis=0
        )
        x = last(x, inv)
        sums = [jnp.zeros((tall, side), jnp.float32)] * 2
        for m in range(modes):
            new_real = x[m * tall : (m + 1) * tall, :side]
            new_imag = x[m * tall : (m + 1) * tall, side:]
            real, imag = (rolled[h, m, :, part, :].reshape(tall, side) for h in range(2))
            sums[0] += real * new_real + imag * new_imag
            sums[1] += real * new_imag - imag * new_real
        for h in range(2):
            terms[h, :, part, :] = sums[h].reshape(layers, step, side)
        pl.when(has_right)(rights[k].start)

    def share_out(k):
        part = parts[k]
        at = line + k * step
        for h in range(2):
            mine = jnp.where(lane >= over, terms[h, :, part, :], 0.0)
            own[h, :, part, :] = jnp.where(at >= down, mine, 0.0)
            lower[h, :, part, :] = jnp.where(at < down, mine, 0.0)

        @pl.when(has_left)
        def _():
            rights[k].wait_recv()
            for h in range(2):
                other = jnp.where(lane < left_over, left[h, :, part, :], 0.0)
                own[h, :, part, :] += jnp.where(at >= left_down, other, 0.0)
                lower[h, :, part, :] += jnp.where(at < left_down, other, 0.0)

        pl.when(has_below)(downs[k].start)

        @pl.when(jnp.logical_not(has_above))
        def _():
            for copy in spreads[k]:
                copy.start()

    def finish(k):
        part = parts[k]
        for copy in spreads[k]:
            copy.wait_recv()
        for h in range(2):
            number = own[h, l, part, :] + DAMPING * obj[h, l, part, :]
            for d in range(1, layers):
                number += shares[d, h, part, :]
            out[h, l, part, :] = number / weight[part, :]
        for copy in gathers[k]:
            copy.start()

    for k in range(count + LAG):
        if k < count:
            rows_back(k)
        if k >= LAG:
            share_out(k - LAG)

    across_share = lax.broadcasted_iota(jnp.int32, (share, side), 1)
    along_share = lax.broadcasted_iota(jnp.int32, (share, side), 0) + l * share
    weight[...] = jnp.full_like(weight, DAMPING)
    there = (None, has_left, has_above, has_left & has_above)
    for group in range(4):

        def add(layer, carry, group=group):
            a, b = corner_of(corners, group, layer, side)
            window = turned(power[...], a, 0).reshape(layers, share, side)
            rows_of[...] = window
            window = rows_of[l]
            window = turned(window, b, 1)
            keep = (along_share < a) if group >= 2 else (along_share >= a)
            keep &= (across_share < b) if group % 2 else (across_share >= b)
            weight[...] += jnp.where(keep, window, 0.0)
            return carry

        def all_layers(add=add):
            lax.fori_loop(0, layers, add, 0)

        if there[group] is None:
            all_layers()
        else:
            pl.when(there[group])(all_layers)

    @pl.when(has_above)
    def _():
        for k, part in enumerate(parts):
            downs[k].wait_recv()
            for h in range(2):
                own[h, :, part, :] += upper[h, :, part, :]
            for copy in spreads[k]:
                copy.start()
            if k >= 2:
                finish(k - 2)
        for k in range(max(count - 2, 0), count):
            finish(k)

    @pl.when(jnp.logical_not(has_above))
    def _():
        for k in range(count):
            finish(k)

    for k in range(count):
        for copy in gathers[k]:
            copy.wait()
        for copy in spreads[k]:
            copy.wait_send()

    @pl.when(has_left)
    def _():
        for copy in lefts:
            copy.wait_send()

    @pl.when(has_above)
    def _():
        for copy in ups:
            copy.wait_send()

    @pl.when(has_right)
    def _():
        across.wait_send()
        for copy in rights:
            copy.wait_send()

    @pl.when(has_below)
    def _():
        down0.wait_send()
        for copy in downs:
            copy.wait_send()

    @pl.when(has_below & has_left)
    def _():
        down1.wait_send()
        for copy in diags:
            copy.wait_send()


def tables(side):
    steps = np.arange(side)
    angle = (steps[:, None] * steps[None, :] % side) * (2.0 * np.pi / side)
    real, imag = np.cos(angle) / np.sqrt(side), -np.sin(angle) / np.sqrt(side)
    both = np.block([[real, imag], [-imag, real]])

    def halves(x):
        x = x.astype(np.float32)
        high = x.astype(jnp.bfloat16)
        return high, (x - high.astype(np.float32)).astype(jnp.bfloat16)

    return halves(both) + halves(both.T)


def body(sizes, object_field, probe_modes, amplitudes, offsets):
    rows, cols, layers = sizes
    side = object_field.shape[1]
    assert object_field.shape[2] == side and probe_modes.shape[2] == side
    assert offsets.shape[0] == 1 and side % (8 * layers) == 0
    modes = probe_modes.shape[1]
    vmem = pl.BlockSpec(memory_space=pltpu.VMEM)
    smem = pl.BlockSpec(memory_space=pltpu.SMEM)
    pair = (2, side, side)
    f32 = jnp.float32
    dma = pltpu.SemaphoreType.DMA
    share = side // layers
    count = min(PIECES, share // 8)
    cut = (2, layers, share, side)
    tabs = tuple(jnp.asarray(t) for t in tables(side))
    tab = pltpu.VMEM((2 * side, 2 * side), jnp.bfloat16)
    probe_cut = (2, modes, layers, share, side)
    whole = pltpu.VMEM(cut, f32)
    corners = (4, layers, 1, 128)
    new_object = pl.pallas_call(
        functools.partial(kernel, sizes),
        out_shape=jax.ShapeDtypeStruct(cut, f32),
        in_specs=[smem, vmem] + [pl.BlockSpec(memory_space=pl.ANY)] * 6,
        out_specs=vmem,
        scratch_shapes=[pltpu.VMEM(probe_cut, f32), pltpu.VMEM((1, side, side), f32)]
        + [tab] * 4
        + [pltpu.VMEM(corners, jnp.int32), pltpu.SMEM(corners, jnp.int32)]
        + [whole] * 3
        + [
            pltpu.VMEM(probe_cut, f32),
            pltpu.VMEM((modes, layers, share, 2 * side), f32),
            pltpu.VMEM((modes, 2 * side, side), f32),
            pltpu.VMEM((side, side), f32),
            pltpu.VMEM((side, side), f32),
            pltpu.VMEM((share, side), f32),
            pltpu.VMEM(cut[1:], f32),
        ]
        + [whole] * 5
        + [pltpu.VMEM((layers, 2, share, side), f32)]
        + [dma((6,)), dma(())]
        + [dma((layers,))] * 2
        + [dma((3,))] * 2
        + [dma((count,))] * 10
        + [dma((count, layers))] * 4,
        compiler_params=pltpu.CompilerParams(
            collective_id=0, has_side_effects=True, vmem_limit_bytes=60 * 1024 * 1024
        ),
        name="update",
    )(
        offsets,
        object_field.reshape(cut),
        probe_modes.reshape(probe_cut),
        amplitudes,
        *tabs,
    )
    return new_object.reshape(pair)


def solution(mesh):
    sizes = tuple(mesh.shape[a] for a in AXES)
    placed = (
        P(None, "row", "col"),
        P(),
        P(("row", "col", "layer"), None, None),
        P(("row", "col", "layer"), None),
    )
    return jax.shard_map(
        functools.partial(body, sizes),
        mesh=mesh,
        in_specs=placed,
        out_specs=P(None, "row", "col"),
        check_vma=False,
    )
```

time: 75.4 us -> 65.6 us (0.87)
  Pallas kernels: 73.3 us -> 63.5 us
    pallas_call x3 -> x1, Pallas kernels: 73.3 us -> 63.5 us  [body(): pl.pallas_call(functools.partial(kernel, sizes), out_shape=jax.ShapeDtype...]
where the time goes in v2:
time: 65.6 us; the launch traced here: 65.4 us
  Pallas kernels  63.5 us (97%)
  local copies, waits for them, and re-layouts  1.87 us (3%)
    pallas_call x1, Pallas kernels, body(): pl.pallas_call(functools.partial(kernel, sizes), out_shape=jax.ShapeDtype...  63.5 us
    unnamed x1, local copies, waits for them, and re-layouts  1.87 us

profile of v2, /device:TPU:6, one launch (start us, length us, event | category | flops | bytes accessed | tf_op | source)
XLA Modules:
  0.0 65.4 jit_solution(16248248760500655864)
XLA Ops:
  0.0 63.5 %update.1 = f32[2,4,64,256]{3,2,1,0:T(8,128)} custom-call(s32[1,2]{1,0:T(1,128)} %corner.1, f32[2,4,64,256]{3,2,1,0:T(8,128)} %bitcast.5, f32[2,4,4,64,256]{4,3,2,1,0:T(8,128)} %bitcast.3, f32[1,256,256]{2,1,0:T(8,128)} %amp_hbm.1, bf16[512,512]{1,0:T(8,128)(2,1)} %constant.8.clone.fwd_high_hbm, bf16[512,512]{1,0:T(8,128)(2,1)} %constant.9.clone.fwd_low_hbm, ...), custom_call_target="tpu_custom_call" | custom-call | tf_op jit(solution)/shard_map/update/pallas_call | solution.py:474
  63.5 1.9 %copy.10 = f32[2,256,256]{2,1,0:T(8,128)} copy(f32[2,256,256]{2,1,0:T(8,128)} %bitcast.4) | data formatting | bytes 1048576

commit v3 on v2

--- a/solution.py
+++ b/solution.py
@@ -68,12 +68,7 @@
 
 
 def turned(x, amount, axis):
-    length = x.shape[axis]
-    bit = 1
-    while bit < length:
-        x = jnp.where(lax.rem(lax.div(amount, bit), 2) == 1, jnp.roll(x, bit, axis), x)
-        bit *= 2
-    return x
+    return pltpu.roll(x, amount, axis)
 
 
 def corner_of(offs, group, layer, side):

time: 65.6 us -> 60.5 us (0.922)
  Pallas kernels: 63.5 us -> 58.4 us
    pallas_call x1, Pallas kernels: 63.5 us -> 58.4 us  [body(): pl.pallas_call(functools.partial(kernel, sizes), out_shape=jax.ShapeDtype...]
where the time goes in v3:
time: 60.5 us; the launch traced here: 60.2 us
  Pallas kernels  58.4 us (97%)
  local copies, waits for them, and re-layouts  1.87 us (3%)
    pallas_call x1, Pallas kernels, body(): pl.pallas_call(functools.partial(kernel, sizes), out_shape=jax.ShapeDtype...  58.4 us
    unnamed x1, local copies, waits for them, and re-layouts  1.87 us

profile of v3, /device:TPU:6, one launch (start us, length us, event | category | flops | bytes accessed | tf_op | source)
XLA Modules:
  0.0 60.2 jit_solution(2221724840260380572)
XLA Ops:
  0.0 58.4 %update.1 = f32[2,4,64,256]{3,2,1,0:T(8,128)} custom-call(s32[1,2]{1,0:T(1,128)} %corner.1, f32[2,4,64,256]{3,2,1,0:T(8,128)} %bitcast.5, f32[2,4,4,64,256]{4,3,2,1,0:T(8,128)} %bitcast.3, f32[1,256,256]{2,1,0:T(8,128)} %amp_hbm.1, bf16[512,512]{1,0:T(8,128)(2,1)} %constant.8.clone.fwd_high_hbm, bf16[512,512]{1,0:T(8,128)(2,1)} %constant.9.clone.fwd_low_hbm, ...), custom_call_target="tpu_custom_call" | custom-call | tf_op jit(solution)/shard_map/update/pallas_call | solution.py:469
  58.4 1.9 %copy.10 = f32[2,256,256]{2,1,0:T(8,128)} copy(f32[2,256,256]{2,1,0:T(8,128)} %bitcast.4) | data formatting | bytes 1048576
